TPU v7x, 32 devices: a whole 2x2x4 slice. The times are simulated.
32 devices in a mesh: member: 2 (over x), row: 16 (over z, y, core).
Axes of the slice: x: 2, y: 2, z: 4, core: 2. Of those that a mesh axis runs over, the one named last changes fastest.
Arguments:
- field: float32 [8, 6, 2048, 2048], P('member', None, 'row'), parts along dimension 0, as said below
- host: float32 [128, 2, 8, 6, 128], P('row', None, 'member'), parts along dimension 2, may hold values from -0.12 to 0.12
- weights: float32 [8, 4], replicated, may hold values from 0.1 to 1
- cut_x: int32 [6], replicated, may hold values from 16 to 63
- cut_y: int32 [6], replicated, may hold values from 16 to 63
- table_index: int32 [6], replicated, may hold values from 0 to 7
Outputs:
- nudged: float32 [8, 6, 2048, 2048], P('member', None, 'row'), parts along dimension 0
There are 2 independent parts, one for each index of `member`. A program takes and returns all parts, laid end to end along the dimension named above; an argument that names none is the same for every part. Nothing has to cross between parts.
Inputs may be any that keep to these rules, and one draw needn't show every extreme that they name: `field`: real-valued fields with strong large-scale structure.
All inputs are finite; a program needn't handle non-finite values.
Results may differ from a plain program's by a relative error of at most 0.00005.
Values sent between devices are 32-bit elements; how exact they have to be, the bound alone decides.
A program may use at most 128 MiB of HBM per device.

v0:
```python
import functools
import math

import jax
import jax.numpy as jnp
import numpy as np
from jax import lax
from jax.experimental import pallas as pl
from jax.experimental.pallas import tpu as pltpu
from jax.sharding import PartitionSpec as P

TABLE = 8
MESH = pl.DeviceIdType.MESH
HIGHEST = lax.Precision.HIGHEST


def box_wave(index, khalf):
    half = index // 2
    return jnp.where(index % 2 == 0, half, jnp.where(index == 1, -khalf, -half))


def wave_tables(positions, length, waves):
    phase = jnp.mod(positions[:, None] * waves[None, :], length).astype(jnp.float32) * (
        2.0 * math.pi / length
    )
    return (jnp.cos(phase), jnp.sin(phase))


def scales(weights, cut_x, cut_y, table_index, x_waves, own_waves):
    onehot = (table_index[:, None] == lax.iota(jnp.int32, TABLE)[None, :]).astype(jnp.float32)
    blend = jnp.dot(onehot, weights, precision=HIGHEST)
    mask_x = (jnp.abs(x_waves)[None, :] <= cut_x[:, None]).astype(jnp.float32)
    mask_y = (jnp.abs(own_waves)[:, None] <= cut_y[None, :]).astype(jnp.float32)
    return (
        blend.T[None, :, :, None] * mask_y[:, None, :, None] * mask_x[None, None, :, :]
    )


def general(field, host, weights, cut_x, cut_y, table_index):
    row_count, ny = field.shape[2:]
    owned, kbox = host.shape[0], host.shape[-1]
    devices = lax.axis_size("row")
    nx = row_count * devices
    place = lax.axis_index("row")
    local_rows = place * row_count + lax.iota(jnp.int32, row_count)
    x_waves = lax.iota(jnp.int32, kbox) - kbox // 2
    y_waves = box_wave(lax.iota(jnp.int32, kbox), kbox // 2)
    cos_y, sin_y = wave_tables(lax.iota(jnp.int32, ny), ny, y_waves)
    table_y = jnp.stack([cos_y, -sin_y], 1) / ny
    spread = jnp.einsum("vlxy,yck->kcvlx", field, table_y, precision=HIGHEST)
    cosine, sine = wave_tables(local_rows, nx, x_waves)
    moved = lax.all_to_all(spread, "row", split_axis=0, concat_axis=4, tiled=True)
    cos_all, sin_all = wave_tables(lax.iota(jnp.int32, nx), nx, x_waves)
    cos_all, sin_all = cos_all / nx, sin_all / nx
    table = jnp.stack([jnp.stack([cos_all, -sin_all], 1), jnp.stack([sin_all, cos_all], 1)], 0)
    spectrum = jnp.einsum("kcvlx,cxdq->kdvlq", moved, table, precision=HIGHEST)
    own_waves = box_wave(place * owned + lax.iota(jnp.int32, owned), kbox // 2)
    scale = scales(weights, cut_x, cut_y, table_index, x_waves, own_waves)
    delta = scale[:, None] * (host - spectrum)
    slab = lax.all_gather(delta, "row", axis=0, tiled=True)
    table = jnp.stack([jnp.stack([cosine.T, sine.T], 1), jnp.stack([-sine.T, cosine.T], 1)], 0)
    back = jnp.einsum("kcvlq,cqdx->kdvlx", slab, table, precision=HIGHEST)
    table_back = jnp.stack([cos_y.T, -sin_y.T], 1)
    return field + jnp.einsum("kcvlx,kcy->vlxy", back, table_back, precision=HIGHEST)


def halves(values):
    high = values.astype(jnp.bfloat16)
    return high, (values - high.astype(jnp.float32)).astype(jnp.bfloat16)


def np_halves(values):
    values = values.astype(np.float32)
    high = values.astype(jnp.bfloat16)
    return high, (values - high.astype(np.float32)).astype(jnp.bfloat16)


def real_modes(length, waves, is_sine):
    phase = (np.arange(length)[:, None] * waves[None, :]) % length * (2.0 * np.pi / length)
    return np.where(is_sine[None, :], np.sin(phase), np.cos(phase))


def forward_kernel(rows, field_ref, table_ref, x_ref, out_ref):
    _, count, row_count, ny = field_ref.shape
    kbox = x_ref.shape[1]
    high, low = halves(field_ref[...].reshape(count * row_count, ny))
    both = jnp.dot(high, table_ref[...], preferred_element_type=jnp.float32)
    rest = jnp.dot(low, table_ref[:, :kbox], preferred_element_type=jnp.float32)
    part = both[:, :kbox] + both[:, kbox:] + rest
    for k in range(count):
        moded = lax.dot_general(
            part[k * row_count : (k + 1) * row_count],
            x_ref[...],
            (((0,), (0,)), ((), ())),
            precision=HIGHEST,
            preferred_element_type=jnp.float32,
        )
        out_ref[:, k] = moded.reshape(out_ref.shape[0], rows, kbox)


def inverse_kernel(field_ref, modes_ref, table_ref, x_ref, out_ref):
    _, count, row_count, ny = field_ref.shape
    kbox = x_ref.shape[1]
    parts = [
        lax.dot_general(
            x_ref[...],
            modes_ref[:, k].reshape(kbox, kbox),
            (((1,), (1,)), ((), ())),
            precision=HIGHEST,
            preferred_element_type=jnp.float32,
        )
        for k in range(count)
    ]
    high, low = halves(jnp.concatenate(parts, 0))
    added = jnp.dot(
        jnp.concatenate([high, high], 1), table_ref[...], preferred_element_type=jnp.float32
    )
    added += jnp.dot(low, table_ref[:kbox], preferred_element_type=jnp.float32)
    out_ref[...] = field_ref[...] + added.reshape(field_ref.shape)


def exchange_kernel(
    bits, orders, owned, norm, part_ref, host_ref, scale_ref, mc_ref, ms_ref, out_ref, *scratch
):
    pipes = len(orders)
    got = [scratch[q * bits : (q + 1) * bits] for q in range(pipes)]
    kept = [scratch[(pipes + q) * bits : (pipes + q + 1) * bits] for q in range(pipes)]
    send_sem, recv_sem = scratch[2 * pipes * bits :]
    me = lax.axis_index("row")
    member = lax.axis_index("member")
    mine = [(me // (1 << b)) % 2 for b in range(bits)]
    peer = [me + (1 << b) * (1 - 2 * mine[b]) for b in range(bits)]
    rows = part_ref.shape[-2]
    span = rows // pipes

    barrier = pltpu.get_barrier_semaphore()
    for b in range(bits):
        pl.semaphore_signal(barrier, inc=1, device_id=(member, peer[b]), device_id_type=MESH)
    pl.semaphore_wait(barrier, bits)

    def pick(ref, order, step, flip):
        left = sorted(order[step:], reverse=True)
        bit = order[step]
        index = tuple(
            (1 - mine[bit] if flip else mine[bit]) if b == bit else slice(None) for b in left
        )
        return index

    def reduce_copy(q, step):
        order = orders[q]
        index = pick(None, order, step, True)
        if step == 0:
            source = part_ref.at[index + (pl.ds(q * span, span),)]
        else:
            source = kept[q][step - 1].at[index]
        return pltpu.make_async_remote_copy(
            src_ref=source,
            dst_ref=got[q][step],
            send_sem=send_sem.at[q, step],
            recv_sem=recv_sem.at[q, step],
            device_id=(member, peer[order[step]]),
            device_id_type=MESH,
        )

    copies = [reduce_copy(q, 0) for q in range(pipes)]
    for copy in copies:
        copy.start()
    for step in range(bits):
        for q in range(pipes):
            copies[q].wait()
            index = pick(None, orders[q], step, False)
            if step == 0:
                own = part_ref[index + (pl.ds(q * span, span),)]
            else:
                own = kept[q][step - 1][index]
            kept[q][step][...] = own + got[q][step][...]
            if step + 1 < bits:
                copies[q] = reduce_copy(q, step + 1)
                copies[q].start()

    half = owned // 2
    line = lax.broadcasted_iota(jnp.int32, (span, 1), 0) % owned < half

    def swap(values):
        return jnp.where(
            line, pltpu.roll(values, span - half, 0), pltpu.roll(values, half, 0)
        )

    def mix(values, ref, axis):
        return lax.dot_general(
            values,
            ref[...],
            (((1,), (axis,)), ((), ())),
            precision=HIGHEST,
            preferred_element_type=jnp.float32,
        )

    def gather_copy(q, step):
        order = orders[q]
        fixed = order[: step + 1]
        index = tuple(mine[b] if b in fixed else slice(None) for b in range(bits - 1, -1, -1))
        block = out_ref.at[index + (pl.ds(q * span, span),)]
        return pltpu.make_async_remote_copy(
            src_ref=block,
            dst_ref=block,
            send_sem=send_sem.at[q, bits + step],
            recv_sem=recv_sem.at[q, bits + step],
            device_id=(member, peer[order[step]]),
            device_id_type=MESH,
        )

    own_index = tuple(mine[b] for b in range(bits - 1, -1, -1))
    for q in range(pipes):
        total = kept[q][bits - 1][...] * norm
        even, odd = mix(total, mc_ref, 0), mix(total, ms_ref, 0)
        even_s, odd_s = swap(even), swap(odd)
        real = jnp.where(line, even - odd_s, even_s + odd)
        imag = jnp.where(line, -(odd + even_s), even - odd_s)
        here = pl.ds(q * span, span)
        real = scale_ref[here] * (host_ref[0, here] - real)
        imag = scale_ref[here] * (host_ref[1, here] - imag)
        real_s, imag_s = swap(real), swap(imag)
        cosine = jnp.where(line, real + real_s, imag - imag_s)
        sine = jnp.where(line, -(imag + imag_s), real - real_s)
        out_ref[own_index + (here,)] = mix(cosine, mc_ref, 1) + mix(sine, ms_ref, 1)
        copies[q] = gather_copy(q, bits - 1)
        copies[q].start()
    for step in range(bits - 1, -1, -1):
        for q in range(pipes):
            copies[q].wait()
            if step > 0:
                copies[q] = gather_copy(q, step - 1)
                copies[q].start()


def exchange(part, host, scale, mc, ms, devices, owned, norm):
    bits = devices.bit_length() - 1
    rows, kbox = part.shape[-2:]
    cube = (2,) * bits
    plain = list(range(bits))
    orders = [plain, [0] + plain[2:] + [1]]
    pipes = len(orders)
    sizes = [
        pltpu.VMEM((2,) * (bits - 1 - step) + (rows // pipes, kbox), jnp.float32)
        for step in range(bits)
    ]
    vmem = pl.BlockSpec(memory_space=pltpu.VMEM)
    out = pl.pallas_call(
        functools.partial(exchange_kernel, bits, orders, owned, norm),
        out_shape=jax.ShapeDtypeStruct(cube + (rows, kbox), jnp.float32),
        in_specs=[vmem] * 5,
        out_specs=vmem,
        scratch_shapes=sizes * (2 * pipes)
        + [pltpu.SemaphoreType.DMA((pipes, 2 * bits)), pltpu.SemaphoreType.DMA((pipes, 2 * bits))],
        compiler_params=pltpu.CompilerParams(
            collective_id=0, has_side_effects=True, vmem_limit_bytes=32 * 1024 * 1024
        ),
    )(part.reshape(cube + (rows, kbox)), host, scale, mc, ms)
    return out


def nudge(field, host, weights, cut_x, cut_y, table_index):
    variables, levels, row_count, ny = field.shape
    owned, kbox = host.shape[0], host.shape[-1]
    khalf, half = kbox // 2, owned // 2
    devices = lax.axis_size("row")
    nx = row_count * devices
    place = lax.axis_index("row")
    fields = variables * levels

    column = np.arange(kbox)
    y_wave = column // owned * half + column % half
    y_sine = column % owned >= half
    y_high, y_low = np_halves(real_modes(ny, y_wave, y_sine))
    table_y = jnp.asarray(np.concatenate([y_high, y_low], 1))
    table_back = jnp.asarray(np.concatenate([y_high.T, y_low.T], 0))
    x_all = real_modes(nx, column % khalf, column >= khalf).astype(np.float32)
    table_x = lax.dynamic_slice_in_dim(jnp.asarray(x_all), place * row_count, row_count, 0)
    wave = column - khalf
    inside = np.abs(wave) < khalf
    mc = ((column[:, None] == np.abs(wave)[None, :]) & inside).astype(np.float32)
    ms = ((column[:, None] == np.abs(wave)[None, :] + khalf) & inside) * np.sign(wave)
    ms = ms.astype(np.float32)

    group = math.gcd(levels, 3)
    steps = levels // group
    grid_block = pl.BlockSpec((1, group, row_count, ny), lambda v, g: (v, g, 0, 0))
    mode_block = pl.BlockSpec(
        (devices, group, owned, kbox), lambda v, g: (0, v * steps + g, 0, 0)
    )

    def whole(*shape):
        return pl.BlockSpec(shape, lambda v, g: (0,) * len(shape))

    params = pltpu.CompilerParams(vmem_limit_bytes=48 * 1024 * 1024)
    part = pl.pallas_call(
        functools.partial(forward_kernel, owned),
        grid=(variables, steps),
        out_shape=jax.ShapeDtypeStruct((devices, fields, owned, kbox), jnp.float32),
        in_specs=[grid_block, whole(ny, 2 * kbox), whole(row_count, kbox)],
        out_specs=mode_block,
        compiler_params=params,
    )(field, table_y, table_x)

    row = place * owned + lax.iota(jnp.int32, owned)
    own_waves = box_wave(row, khalf)
    scale = scales(weights, cut_x, cut_y, table_index, lax.iota(jnp.int32, kbox) - khalf, own_waves)
    scale = scale.reshape(half, 2, fields, kbox).transpose(2, 1, 0, 3)
    placed = host.reshape(half, 2, 2, fields, kbox).transpose(2, 3, 1, 0, 4)
    modes = exchange(
        part.reshape(devices, fields * owned, kbox),
        placed.reshape(2, fields * owned, kbox),
        scale.reshape(fields * owned, kbox),
        jnp.asarray(mc),
        jnp.asarray(ms),
        devices,
        owned,
        1.0 / (nx * ny),
    ).reshape(devices, fields, owned, kbox)

    return pl.pallas_call(
        inverse_kernel,
        grid=(variables, steps),
        out_shape=jax.ShapeDtypeStruct(field.shape, jnp.float32),
        in_specs=[grid_block, mode_block, whole(2 * kbox, ny), whole(row_count, kbox)],
        out_specs=grid_block,
        compiler_params=params,
    )(field, modes, table_back, table_x)


def shards(*args):
    khalf = args[1].shape[-1] // 2
    cut_x, cut_y = args[3:5]
    edge = jnp.maximum(jnp.max(cut_x), jnp.max(cut_y)) >= khalf
    return lax.cond(edge, general, nudge, *args)


def solution(mesh):
    return jax.shard_map(
        shards,
        mesh=mesh,
        in_specs=(
            P("member", None, "row", None),
            P("row", None, "member", None, None),
            P(),
            P(),
            P(),
            P(),
        ),
        out_specs=P("member", None, "row", None),
        check_vma=False,
    )
```

profile of v0, /device:TPU:0, one launch (start us, length us, event | category | flops | bytes accessed | tf_op | source)
XLA Modules:
  0.0 103.3 jit_solution(7956699909806033480)
XLA Ops:
  6.5 1.4 %reduce_max.19 = s32[]{:T(128)} reduce(s32[6]{0:T(128)} %param.17, s32[]{:T(128)} %constant.150.clone.1), dimensions={0}, to_apply=%region_1.0 | reduce | flops 5 | bytes 32 | tf_op jit(solution)/shard_map/reduce_max | solution.py:334
  7.9 1.3 %reduce_max.18 = s32[]{:T(128)} reduce(s32[6]{0:T(128)} %param.16, s32[]{:T(128)} %constant.150.clone.1), dimensions={0}, to_apply=%region_0.0 | reduce | flops 5 | bytes 32 | tf_op jit(solution)/shard_map/reduce_max | solution.py:334
  10.5 86.0 %conditional.1 = (f32[4,6,128,2048]{3,2,1,0:T(8,128)}) conditional(s32[]{:T(128)} %convert_element_type.110, ((), f32[4,6,128,2048]{3,2,1,0:T(8,128)}, (), f32[8,2,4,6,128]{4,2,3,1,0:T(4,128)}, s32[6]{0:T(128)}, /*index=5*/f32[8,4]{0,1:T(4,128)}, s32[6]{0:T(128)}, s32[6]{0:T(128)}, (), (), /*index=10*/()) %tuple.11, (s32[6]{0:T(128)}, ...), branch_computations={%region_2.3_spmd, %region_3.4_spmd} | conditional | flops 43509334016 | bytes 155335040 | solution.py:335
  10.6 0.9 convolution_bitcast_fusion
  11.5 0.1 mul.251
  11.6 0.7 compare_convert_fusion
  12.3 0.7 compare_convert_fusion.1
  13.0 0.1 mul.255
  13.1 0.1 copy.39
  13.2 0.1 mul.258
  13.3 0.9 constant_dynamic-slice_fusion.x_ref
  14.2 0.1 broadcast_multiply_fusion.scale_ref
  14.3 1.0 copy.47
  15.3 0.1 copy.38
  15.4 0.0 copy-start.1
  15.4 1.2 %copy-done.1 = bf16[2048,256]{1,0:T(8,128)(2,1)S(1)} copy-done((bf16[2048,256]{1,0:T(8,128)(2,1)S(1)}, bf16[2048,256]{1,0:T(8,128)(2,1)}, u32[]{:S(2)}) %copy-start.1) | copy-done | bytes 1048600 | tf_op jit(solution)/shard_map/cond
  16.6 0.0 copy-start.2
  16.6 0.0 copy-start.3
  16.6 14.8 %branch_0_fun.3 = f32[16,24,8,128]{3,2,1,0:T(8,128)S(1)} custom-call(f32[4,6,128,2048]{3,2,1,0:T(8,128)} %get-tuple-element.42.field_ref, bf16[2048,256]{1,0:T(8,128)(2,1)S(1)} %copy-done.1, f32[128,128]{1,0:T(8,128)S(1)} %constant_dynamic-slice_fusion.x_ref), custom_call_target="tpu_custom_call" | custom-call | tf_op jit(solution)/shard_map/cond/branch_0_fun/pallas_call | solution.py:296
  31.4 0.0 copy-start
  31.4 0.0 copy-done.2
  31.4 0.0 copy-done.3
  31.5 41.0 %branch_0_fun.4 = f32[2,2,2,2,192,128]{5,4,3,2,1,0:T(8,128)S(1)} custom-call(f32[2,2,2,2,192,128]{5,4,3,2,1,0:T(8,128)S(1)} %bitcast.82, f32[2,192,128]{2,1,0:T(8,128)S(1)} %bitcast.83, f32[192,128]{1,0:T(8,128)S(1)} %broadcast_multiply_fusion.scale_ref, f32[128,128]{1,0:T(8,128)S(1)} %copy-done.3, f32[128,128]{1,0:T(8,128)S(1)} %copy-done.2), custom_call_target="tpu_custom_call" | custom-call | tf_op jit(solution)/shard_map/cond/branch_0_fun/pallas_call | solution.py:248
  72.5 0.0 copy-done
  72.5 24.0 %branch_0_fun.5 = f32[4,6,128,2048]{3,2,1,0:T(8,128)} custom-call(f32[4,6,128,2048]{3,2,1,0:T(8,128)} %get-tuple-element.42.field_ref, f32[16,24,8,128]{3,2,1,0:T(8,128)S(1)} %bitcast.81, bf16[256,2048]{1,0:T(8,128)(2,1)S(1)} %copy-done, f32[128,128]{1,0:T(8,128)S(1)} %constant_dynamic-slice_fusion.x_ref), custom_call_target="tpu_custom_call" | custom-call | tf_op jit(solution)/shard_map/cond/branch_0_fun/pallas_call | solution.py:321
  (7 shorter events, 0.1 us)
Async XLA Ops:
  15.4 1.2 %copy-start.1 = (bf16[2048,256]{1,0:T(8,128)(2,1)S(1)}, bf16[2048,256]{1,0:T(8,128)(2,1)}, u32[]{:S(2)}) copy-start(bf16[2048,256]{1,0:T(8,128)(2,1)} %constant.152.clone.1.table_ref) | copy-start | bytes 3145732 | tf_op jit(solution)/shard_map/cond
  16.6 14.8 %copy-start.2 = (f32[128,128]{1,0:T(8,128)S(1)}, f32[128,128]{1,0:T(8,128)}, u32[]{:S(2)}) copy-start(f32[128,128]{1,0:T(8,128)} %constant.156.clone.1.ms_ref) | copy-start | bytes 196612 | tf_op jit(solution)/shard_map/cond
  16.6 14.8 %copy-start.3 = (f32[128,128]{1,0:T(8,128)S(1)}, f32[128,128]{1,0:T(8,128)}, u32[]{:S(2)}) copy-start(f32[128,128]{1,0:T(8,128)} %constant.155.clone.1.mc_ref) | copy-start | bytes 196612 | tf_op jit(solution)/shard_map/cond
  31.4 41.1 %copy-start = (bf16[256,2048]{1,0:T(8,128)(2,1)S(1)}, bf16[256,2048]{1,0:T(8,128)(2,1)}, u32[]{:S(2)}) copy-start(bf16[256,2048]{1,0:T(8,128)(2,1)} %constant.153.clone.1.table_ref) | copy-start | bytes 3145732 | tf_op jit(solution)/shard_map/cond
where the time goes:
time: 104 us; the launch traced here: 103 us
  Pallas kernels  79.8 us (77%)
  between operations  14.7 us (14%)
  other arithmetic  4.23 us (4%)
  local copies, waits for them, and re-layouts  3.54 us (3%)
    pallas_call x1, Pallas kernels, exchange(): pl.pallas_call(functools.partial(exchange_kernel, bits, orders, owned, no...  41 us
    pallas_call x1, Pallas kernels, nudge(): pl.pallas_call(inverse_kernel, grid=(variables, steps), out_shape=jax.Sha...  24 us
    pallas_call x1, Pallas kernels, nudge(): pl.pallas_call(functools.partial(forward_kernel, owned), grid=(variables,...  14.8 us
    reduce_max x2, other arithmetic, shards(): edge = jnp.maximum(jnp.max(cut_x), jnp.max(cut_y)) >= khalf  2.66 us

commit v1 on v0

--- a/solution.py
+++ b/solution.py
@@ -26,42 +26,44 @@
     return (jnp.cos(phase), jnp.sin(phase))
 
 
-def scales(weights, cut_x, cut_y, table_index, x_waves, own_waves):
-    onehot = (table_index[:, None] == lax.iota(jnp.int32, TABLE)[None, :]).astype(jnp.float32)
-    blend = jnp.dot(onehot, weights, precision=HIGHEST)
-    mask_x = (jnp.abs(x_waves)[None, :] <= cut_x[:, None]).astype(jnp.float32)
-    mask_y = (jnp.abs(own_waves)[:, None] <= cut_y[None, :]).astype(jnp.float32)
-    return (
-        blend.T[None, :, :, None] * mask_y[:, None, :, None] * mask_x[None, None, :, :]
-    )
-
-
 def general(field, host, weights, cut_x, cut_y, table_index):
-    row_count, ny = field.shape[2:]
+    variables, levels, row_count, ny = field.shape
     owned, kbox = host.shape[0], host.shape[-1]
+    fields = variables * levels
     devices = lax.axis_size("row")
     nx = row_count * devices
     place = lax.axis_index("row")
     local_rows = place * row_count + lax.iota(jnp.int32, row_count)
     x_waves = lax.iota(jnp.int32, kbox) - kbox // 2
     y_waves = box_wave(lax.iota(jnp.int32, kbox), kbox // 2)
+    own_waves = box_wave(place * owned + lax.iota(jnp.int32, owned), kbox // 2)
+    onehot = (table_index[:, None] == lax.iota(jnp.int32, TABLE)[None, :]).astype(jnp.float32)
+    blend = jnp.dot(onehot, weights, precision=HIGHEST)
+    mask_x = (jnp.abs(x_waves)[None, :] <= cut_x[:, None]).astype(jnp.float32)
+    mask_y = (jnp.abs(own_waves)[None, :] <= cut_y[:, None]).astype(jnp.float32)
+    scale = blend.T[:, :, None, None] * mask_y[None, :, :, None] * mask_x[None, :, None, :]
     cos_y, sin_y = wave_tables(lax.iota(jnp.int32, ny), ny, y_waves)
-    table_y = jnp.stack([cos_y, -sin_y], 1) / ny
-    spread = jnp.einsum("vlxy,yck->kcvlx", field, table_y, precision=HIGHEST)
-    cosine, sine = wave_tables(local_rows, nx, x_waves)
-    moved = lax.all_to_all(spread, "row", split_axis=0, concat_axis=4, tiled=True)
-    cos_all, sin_all = wave_tables(lax.iota(jnp.int32, nx), nx, x_waves)
-    cos_all, sin_all = cos_all / nx, sin_all / nx
-    table = jnp.stack([jnp.stack([cos_all, -sin_all], 1), jnp.stack([sin_all, cos_all], 1)], 0)
-    spectrum = jnp.einsum("kcvlx,cxdq->kdvlq", moved, table, precision=HIGHEST)
-    own_waves = box_wave(place * owned + lax.iota(jnp.int32, owned), kbox // 2)
-    scale = scales(weights, cut_x, cut_y, table_index, x_waves, own_waves)
-    delta = scale[:, None] * (host - spectrum)
-    slab = lax.all_gather(delta, "row", axis=0, tiled=True)
-    table = jnp.stack([jnp.stack([cosine.T, sine.T], 1), jnp.stack([-sine.T, cosine.T], 1)], 0)
-    back = jnp.einsum("kcvlq,cqdx->kdvlx", slab, table, precision=HIGHEST)
-    table_back = jnp.stack([cos_y.T, -sin_y.T], 1)
-    return field + jnp.einsum("kcvlx,kcy->vlxy", back, table_back, precision=HIGHEST)
+    cos_x, sin_x = wave_tables(local_rows, nx, x_waves)
+    table_y = jnp.concatenate([cos_y, -sin_y], 1)
+    table_x = jnp.stack([jnp.concatenate([cos_x, -sin_x], 1), jnp.concatenate([sin_x, cos_x], 1)])
+
+    def one(pair):
+        grid, wanted, factor = pair
+        spread = jnp.dot(grid, table_y, precision=HIGHEST).reshape(row_count, 2, kbox)
+        parts = jnp.einsum("xck,cxq->kq", spread, table_x, precision=HIGHEST)
+        parts = parts.reshape(devices, owned, 2, kbox)
+        moved = lax.all_to_all(parts, "row", split_axis=0, concat_axis=0, tiled=True)
+        spectrum = jnp.sum(moved, 0) / (nx * ny)
+        delta = factor[:, None, :] * (wanted - spectrum)
+        box = lax.all_gather(delta, "row", axis=0, tiled=True).reshape(kbox, 2 * kbox)
+        back = jnp.einsum("kq,cxq->xck", box, table_x, precision=HIGHEST)
+        return grid + jnp.dot(back.reshape(row_count, 2 * kbox), table_y.T, precision=HIGHEST)
+
+    wanted = host.transpose(2, 3, 0, 1, 4).reshape(fields, owned, 2, kbox)
+    result = lax.map(
+        one, (field.reshape(fields, row_count, ny), wanted, scale.reshape(fields, owned, kbox))
+    )
+    return result.reshape(field.shape)
 
 
 def halves(values):
@@ -75,57 +77,79 @@
     return high, (values - high.astype(np.float32)).astype(jnp.bfloat16)
 
 
-def real_modes(length, waves, is_sine):
-    phase = (np.arange(length)[:, None] * waves[None, :]) % length * (2.0 * np.pi / length)
+def real_modes(positions, length, waves, is_sine):
+    if isinstance(positions, int):
+        positions = np.arange(positions)
+    phase = (positions[:, None] * waves[None, :]) % length * (2.0 * np.pi / length)
     return np.where(is_sine[None, :], np.sin(phase), np.cos(phase))
 
 
-def forward_kernel(rows, field_ref, table_ref, x_ref, out_ref):
+def local_modes(base_ref, turn_ref):
+    count = base_ref.shape[0] // 2
+    return base_ref[:count] * turn_ref[0, :1] + base_ref[count:] * turn_ref[0, 1:2]
+
+
+def forward_kernel(owned, cut_x_ref, cut_y_ref, field_ref, table_ref, base_ref, turn_ref, out_ref, edge_ref):
     _, count, row_count, ny = field_ref.shape
-    kbox = x_ref.shape[1]
+    kbox = base_ref.shape[1]
+    edge = cut_x_ref[0]
+    for level in range(cut_x_ref.shape[0]):
+        edge = jnp.maximum(edge, jnp.maximum(cut_x_ref[level], cut_y_ref[level]))
+    edge_ref[0] = edge
     high, low = halves(field_ref[...].reshape(count * row_count, ny))
     both = jnp.dot(high, table_ref[...], preferred_element_type=jnp.float32)
     rest = jnp.dot(low, table_ref[:, :kbox], preferred_element_type=jnp.float32)
     part = both[:, :kbox] + both[:, kbox:] + rest
+    x_high, x_low = halves(local_modes(base_ref, turn_ref))
+    x_three = jnp.concatenate([x_high, x_high, x_low], 0)
     for k in range(count):
+        high, low = halves(part[k * row_count : (k + 1) * row_count])
         moded = lax.dot_general(
-            part[k * row_count : (k + 1) * row_count],
-            x_ref[...],
+            jnp.concatenate([high, low, high], 0),
+            x_three,
             (((0,), (0,)), ((), ())),
-            precision=HIGHEST,
             preferred_element_type=jnp.float32,
         )
-        out_ref[:, k] = moded.reshape(out_ref.shape[0], rows, kbox)
-
-
-def inverse_kernel(field_ref, modes_ref, table_ref, x_ref, out_ref):
+        out_ref[:, k] = moded.reshape(out_ref.shape[0], owned, kbox)
+
+
+def inverse_kernel(field_ref, modes_ref, table_ref, base_ref, turn_ref, out_ref, three_ref):
     _, count, row_count, ny = field_ref.shape
-    kbox = x_ref.shape[1]
-    parts = [
-        lax.dot_general(
-            x_ref[...],
-            modes_ref[:, k].reshape(kbox, kbox),
-            (((1,), (1,)), ((), ())),
-            precision=HIGHEST,
-            preferred_element_type=jnp.float32,
-        )
-        for k in range(count)
-    ]
+    kbox = base_ref.shape[1]
+    x_high, x_low = halves(local_modes(base_ref, turn_ref))
+    x_three = jnp.concatenate([x_high, x_high, x_low], 1)
+
+    @pl.when((pl.program_id(0) == 0) & (pl.program_id(1) == 0))
+    def _():
+        three_ref[:kbox] = table_ref[:kbox]
+        three_ref[kbox:] = table_ref[...]
+
+    parts = []
+    for k in range(count):
+        high, low = halves(modes_ref[:, k].reshape(kbox, kbox))
+        parts.append(
+            lax.dot_general(
+                x_three,
+                jnp.concatenate([high, low, high], 1),
+                (((1,), (1,)), ((), ())),
+                preferred_element_type=jnp.float32,
+            )
+        )
     high, low = halves(jnp.concatenate(parts, 0))
     added = jnp.dot(
-        jnp.concatenate([high, high], 1), table_ref[...], preferred_element_type=jnp.float32
-    )
-    added += jnp.dot(low, table_ref[:kbox], preferred_element_type=jnp.float32)
+        jnp.concatenate([high, low, high], 1), three_ref[...], preferred_element_type=jnp.float32
+    )
     out_ref[...] = field_ref[...] + added.reshape(field_ref.shape)
 
 
 def exchange_kernel(
-    bits, orders, owned, norm, part_ref, host_ref, scale_ref, mc_ref, ms_ref, out_ref, *scratch
+    bits, orders, owned, norm, weights_ref, cut_x_ref, cut_y_ref, index_ref,
+    part_ref, host_ref, mc_ref, ms_ref, out_ref, *scratch
 ):
     pipes = len(orders)
     got = [scratch[q * bits : (q + 1) * bits] for q in range(pipes)]
     kept = [scratch[(pipes + q) * bits : (pipes + q + 1) * bits] for q in range(pipes)]
-    send_sem, recv_sem = scratch[2 * pipes * bits :]
+    scale_ref, send_sem, recv_sem = scratch[2 * pipes * bits :]
     me = lax.axis_index("row")
     member = lax.axis_index("member")
     mine = [(me // (1 << b)) % 2 for b in range(bits)]
@@ -165,6 +189,23 @@
     copies = [reduce_copy(q, 0) for q in range(pipes)]
     for copy in copies:
         copy.start()
+
+    kbox = part_ref.shape[-1]
+    half, khalf = owned // 2, kbox // 2
+    row = lax.broadcasted_iota(jnp.int32, (rows, kbox), 0)
+    column = lax.broadcasted_iota(jnp.int32, (rows, kbox), 1)
+    line_of, slot = row // owned, row % owned
+    wave = me * half + slot % half
+    wave = jnp.where((wave == 0) & (slot >= half), khalf, wave)
+    levels = cut_x_ref.shape[0]
+    scale = jnp.zeros((rows, kbox), jnp.float32)
+    for level in range(levels):
+        kept_wave = (jnp.abs(column - khalf) <= cut_x_ref[level]) & (wave <= cut_y_ref[level])
+        for v in range(rows // owned // levels):
+            blend = jnp.where(kept_wave, weights_ref[index_ref[level], v], 0.0)
+            scale = jnp.where(line_of == v * levels + level, blend, scale)
+    scale_ref[...] = scale
+
     for step in range(bits):
         for q in range(pipes):
             copies[q].wait()
@@ -178,7 +219,6 @@
                 copies[q] = reduce_copy(q, step + 1)
                 copies[q].start()
 
-    half = owned // 2
     line = lax.broadcasted_iota(jnp.int32, (span, 1), 0) % owned < half
 
     def swap(values):
@@ -233,7 +273,7 @@
                 copies[q].start()
 
 
-def exchange(part, host, scale, mc, ms, devices, owned, norm):
+def exchange(scalars, part, host, mc, ms, devices, owned, norm):
     bits = devices.bit_length() - 1
     rows, kbox = part.shape[-2:]
     cube = (2,) * bits
@@ -248,14 +288,15 @@
     out = pl.pallas_call(
         functools.partial(exchange_kernel, bits, orders, owned, norm),
         out_shape=jax.ShapeDtypeStruct(cube + (rows, kbox), jnp.float32),
-        in_specs=[vmem] * 5,
+        in_specs=[pl.BlockSpec(memory_space=pltpu.SMEM)] * 4 + [vmem] * 4,
         out_specs=vmem,
         scratch_shapes=sizes * (2 * pipes)
+        + [pltpu.VMEM((rows, kbox), jnp.float32)]
         + [pltpu.SemaphoreType.DMA((pipes, 2 * bits)), pltpu.SemaphoreType.DMA((pipes, 2 * bits))],
         compiler_params=pltpu.CompilerParams(
             collective_id=0, has_side_effects=True, vmem_limit_bytes=32 * 1024 * 1024
         ),
-    )(part.reshape(cube + (rows, kbox)), host, scale, mc, ms)
+    )(*scalars, part.reshape(cube + (rows, kbox)), host, mc, ms)
     return out
 
 
@@ -265,17 +306,26 @@
     khalf, half = kbox // 2, owned // 2
     devices = lax.axis_size("row")
     nx = row_count * devices
-    place = lax.axis_index("row")
     fields = variables * levels
 
     column = np.arange(kbox)
     y_wave = column // owned * half + column % half
     y_sine = column % owned >= half
-    y_high, y_low = np_halves(real_modes(ny, y_wave, y_sine))
+    y_high, y_low = np_halves(real_modes(ny, ny, y_wave, y_sine))
     table_y = jnp.asarray(np.concatenate([y_high, y_low], 1))
     table_back = jnp.asarray(np.concatenate([y_high.T, y_low.T], 0))
-    x_all = real_modes(nx, column % khalf, column >= khalf).astype(np.float32)
-    table_x = lax.dynamic_slice_in_dim(jnp.asarray(x_all), place * row_count, row_count, 0)
+    x_wave, x_sine = column % khalf, column >= khalf
+    start = np.arange(devices) * row_count
+    base = np.concatenate(
+        [real_modes(row_count, nx, x_wave, column < 0), real_modes(row_count, nx, x_wave, column >= 0)]
+    )
+    turn_cos = real_modes(start, nx, x_wave, column < 0)
+    turn_sin = real_modes(start, nx, x_wave, column >= 0)
+    turn = np.stack(
+        [np.where(x_sine, turn_sin, turn_cos), np.where(x_sine, turn_cos, -turn_sin)], 1
+    )
+    base = jnp.asarray(base.astype(np.float32))
+    turn = jnp.asarray(turn.astype(np.float32))
     wave = column - khalf
     inside = np.abs(wave) < khalf
     mc = ((column[:, None] == np.abs(wave)[None, :]) & inside).astype(np.float32)
@@ -292,25 +342,26 @@
     def whole(*shape):
         return pl.BlockSpec(shape, lambda v, g: (0,) * len(shape))
 
+    local_turn = pl.BlockSpec((1, 2, kbox), lambda v, g: (lax.axis_index("row"), 0, 0))
+    scalar = pl.BlockSpec(memory_space=pltpu.SMEM)
     params = pltpu.CompilerParams(vmem_limit_bytes=48 * 1024 * 1024)
-    part = pl.pallas_call(
+    part, edge = pl.pallas_call(
         functools.partial(forward_kernel, owned),
         grid=(variables, steps),
-        out_shape=jax.ShapeDtypeStruct((devices, fields, owned, kbox), jnp.float32),
-        in_specs=[grid_block, whole(ny, 2 * kbox), whole(row_count, kbox)],
-        out_specs=mode_block,
+        out_shape=(
+            jax.ShapeDtypeStruct((devices, fields, owned, kbox), jnp.float32),
+            jax.ShapeDtypeStruct((1,), jnp.int32),
+        ),
+        in_specs=[scalar, scalar, grid_block, whole(ny, 2 * kbox), whole(2 * row_count, kbox), local_turn],
+        out_specs=(mode_block, scalar),
         compiler_params=params,
-    )(field, table_y, table_x)
-
-    row = place * owned + lax.iota(jnp.int32, owned)
-    own_waves = box_wave(row, khalf)
-    scale = scales(weights, cut_x, cut_y, table_index, lax.iota(jnp.int32, kbox) - khalf, own_waves)
-    scale = scale.reshape(half, 2, fields, kbox).transpose(2, 1, 0, 3)
+    )(cut_x, cut_y, field, table_y, base, turn)
+
     placed = host.reshape(half, 2, 2, fields, kbox).transpose(2, 3, 1, 0, 4)
     modes = exchange(
+        (weights, cut_x, cut_y, table_index),
         part.reshape(devices, fields * owned, kbox),
         placed.reshape(2, fields * owned, kbox),
-        scale.reshape(fields * owned, kbox),
         jnp.asarray(mc),
         jnp.asarray(ms),
         devices,
@@ -318,26 +369,26 @@
         1.0 / (nx * ny),
     ).reshape(devices, fields, owned, kbox)
 
-    return pl.pallas_call(
+    inverse = pl.pallas_call(
         inverse_kernel,
         grid=(variables, steps),
         out_shape=jax.ShapeDtypeStruct(field.shape, jnp.float32),
-        in_specs=[grid_block, mode_block, whole(2 * kbox, ny), whole(row_count, kbox)],
+        in_specs=[grid_block, mode_block, whole(2 * kbox, ny), whole(2 * row_count, kbox), local_turn],
         out_specs=grid_block,
+        scratch_shapes=[pltpu.VMEM((3 * kbox, ny), jnp.bfloat16)],
         compiler_params=params,
-    )(field, modes, table_back, table_x)
-
-
-def shards(*args):
-    khalf = args[1].shape[-1] // 2
-    cut_x, cut_y = args[3:5]
-    edge = jnp.maximum(jnp.max(cut_x), jnp.max(cut_y)) >= khalf
-    return lax.cond(edge, general, nudge, *args)
+    )
+    return lax.cond(
+        edge[0] >= khalf,
+        lambda *args: general(*args[:6]),
+        lambda *args: inverse(args[0], *args[6:]),
+        field, host, weights, cut_x, cut_y, table_index, modes, table_back, base, turn,
+    )
 
 
 def solution(mesh):
     return jax.shard_map(
-        shards,
+        nudge,
         mesh=mesh,
         in_specs=(
             P("member", None, "row", None),

time: 104 us -> 82.9 us (0.80)
  between operations: 14.7 us -> 0.77 us
  other arithmetic: 4.23 us -> 0 us
    reduce_max x2 -> x0, other arithmetic: 2.66 us -> none  [shards(): edge = jnp.maximum(jnp.max(cut_x), jnp.max(cut_y)) >= khalf]
    pallas_call x1, Pallas kernels: 24 us -> 21.8 us  [nudge(): inverse(args[0], *args[6:])]
    convert_element_type x2 -> x0, other arithmetic: 1.46 us -> none  [the longest x1 0.74 us: scales(): mask_x = (jnp.abs(x_waves)[None, :] <= cut_x[:, None]).astype(jnp.float32)]
    unnamed x0 -> x22, local copies, waits for them, and re-layouts: none -> 1.41 us
where the time goes in v1:
time: 82.9 us; the launch traced here: 82.5 us
  Pallas kernels  79 us (95%)
  local copies, waits for them, and re-layouts  2.69 us (3%)
    pallas_call x1, Pallas kernels, exchange(): pl.pallas_call(functools.partial(exchange_kernel, bits, orders, owned, no...  41.6 us
    pallas_call x1, Pallas kernels, nudge(): inverse(args[0], *args[6:])  21.8 us
    pallas_call x1, Pallas kernels, nudge(): pl.pallas_call(functools.partial(forward_kernel, owned), grid=(variables,...  15.5 us

profile of v1, /device:TPU:0, one launch (start us, length us, event | category | flops | bytes accessed | tf_op | source)
XLA Modules:
  0.0 82.5 jit_solution(1860533932539273976)
XLA Ops:
  0.0 0.0 copy-start
  0.0 1.2 %copy-done = bf16[2048,256]{1,0:T(8,128)(2,1)S(1)} copy-done((bf16[2048,256]{1,0:T(8,128)(2,1)S(1)}, bf16[2048,256]{1,0:T(8,128)(2,1)}, u32[]{:S(2)}) %copy-start) | copy-done | bytes 1048600
  1.2 0.0 copy-start.4
  1.2 0.0 copy-start.9
  1.2 0.0 copy-start.2
  1.2 0.0 copy-start.3
  1.2 0.0 copy-start.7
  1.2 0.0 copy-start.8
  1.3 0.0 copy-start.10
  1.3 0.0 copy-start.5
  1.3 0.0 copy-start.6
  1.3 15.5 %shard_map.121 = (f32[16,24,8,128]{3,2,1,0:T(8,128)S(1)}, s32[1]{0:T(128)}) custom-call(s32[6]{0:T(128)} %cut_x_ref.3, s32[6]{0:T(128)} %cut_y_ref.3, f32[4,6,128,2048]{3,2,1,0:T(8,128)} %field_ref.1, bf16[2048,256]{1,0:T(8,128)(2,1)S(1)} %copy-done, f32[256,128]{1,0:T(8,128)} %constant.125.clone.base_ref, f32[16,2,128]{2,1,0:T(2,128)} %constant.126.clone.turn_ref), custom_call_target="tpu_custom_call" | custom-call | tf_op jit(solution)/shard_map/pallas_call | solution.py:348
  16.8 0.0 copy-done.4
  16.8 0.1 copy.26
  16.9 0.1 copy.27
  16.9 0.0 copy-done.9
  16.9 0.1 copy.28.weights_ref
  17.0 0.0 copy-done.2
  17.0 0.0 copy-done.3
  17.0 0.0 copy-done.7
  17.0 0.0 copy-done.8
  17.0 0.0 copy-done.10
  17.1 41.6 %shard_map.122 = f32[2,2,2,2,192,128]{5,4,3,2,1,0:T(8,128)S(1)} custom-call(f32[8,4]{1,0:T(8,128)S(1)} %copy.28.weights_ref, s32[6]{0:T(128)S(1)} %copy-done.7, s32[6]{0:T(128)S(1)} %copy-done.8, s32[6]{0:T(128)S(1)} %copy-done.10, f32[2,2,2,2,192,128]{5,4,3,2,1,0:T(8,128)S(1)} %bitcast.83, f32[2,192,128]{2,1,0:T(8,128)S(1)} %bitcast.84, ...), custom_call_target="tpu_custom_call" | custom-call | tf_op jit(solution)/shard_map/pallas_call | solution.py:288
  59.3 0.0 copy-done.5
  59.4 0.0 copy-done.6
  59.4 23.1 %conditional.1 = (f32[4,6,128,2048]{3,2,1,0:T(8,128)}) conditional(s32[]{:T(128)} %bitcast.19, (f32[4,6,128,2048]{3,2,1,0:T(8,128)}, f32[2,2,2,2,192,128]{5,4,3,2,1,0:T(8,128)S(1)}, (), f32[256,128]{1,0:T(8,128)S(1)}, f32[16,2,128]{2,1,0:T(2,128)S(1)}) %tuple.45, (f32[4,6,128,2048]{3,2,1,0:T(8,128)}, f32[8,2,4,6,128]{4,2,3,1,0:T(4,128)S(1)}, ...), branch_computations={%region_0.0_spmd, %region_1.5_spmd} | conditional | flops 1817103232 | bytes 17667372 | solution.py:381
  59.4 0.0 copy-start.1
  59.4 1.2 %copy-done.1 = bf16[256,2048]{1,0:T(8,128)(2,1)S(1)} copy-done((bf16[256,2048]{1,0:T(8,128)(2,1)S(1)}, bf16[256,2048]{1,0:T(8,128)(2,1)}, u32[]{:S(2)}) %copy-start.1) | copy-done | bytes 1048600 | tf_op jit(solution)/shard_map/cond
  60.6 21.8 %branch_0_fun.1 = f32[4,6,128,2048]{3,2,1,0:T(8,128)} custom-call(f32[4,6,128,2048]{3,2,1,0:T(8,128)} %get-tuple-element.58.field_ref, f32[16,24,8,128]{3,2,1,0:T(8,128)S(1)} %bitcast.89, bf16[256,2048]{1,0:T(8,128)(2,1)S(1)} %copy-done.1, f32[256,128]{1,0:T(8,128)S(1)} %get-tuple-element.61.base_ref, f32[16,2,128]{2,1,0:T(2,128)S(1)} %get-tuple-element.62.turn_ref), custom_call_target="tpu_custom_call" | custom-call | tf_op jit(solution)/shard_map/cond/branch_0_fun/pallas_call | solution.py:384
Async XLA Ops:
  0.0 1.2 %copy-start = (bf16[2048,256]{1,0:T(8,128)(2,1)S(1)}, bf16[2048,256]{1,0:T(8,128)(2,1)}, u32[]{:S(2)}) copy-start(bf16[2048,256]{1,0:T(8,128)(2,1)} %constant.123.clone.table_ref) | copy-start | bytes 3145732
  1.2 15.6 %copy-start.4 = (f32[8,2,4,6,128]{4,2,3,1,0:T(4,128)S(1)}, f32[8,2,4,6,128]{4,2,3,1,0:T(4,128)}, u32[]{:S(2)}) copy-start(f32[8,2,4,6,128]{4,2,3,1,0:T(4,128)} %param.17) | copy-start | bytes 589828
  1.2 15.7 %copy-start.9 = (f32[8,4]{0,1:T(4,128)S(1)}, f32[8,4]{0,1:T(4,128)}, u32[]{:S(2)}) copy-start(f32[8,4]{0,1:T(4,128)} %param.18) | copy-start | bytes 388
  1.2 15.8 %copy-start.2 = (f32[128,128]{1,0:T(8,128)S(1)}, f32[128,128]{1,0:T(8,128)}, u32[]{:S(2)}) copy-start(f32[128,128]{1,0:T(8,128)} %constant.127.clone.mc_ref) | copy-start | bytes 196612
  1.2 15.8 %copy-start.3 = (f32[128,128]{1,0:T(8,128)S(1)}, f32[128,128]{1,0:T(8,128)}, u32[]{:S(2)}) copy-start(f32[128,128]{1,0:T(8,128)} %constant.128.clone.ms_ref) | copy-start | bytes 196612
  1.2 15.8 %copy-start.7 = (s32[6]{0:T(128)S(1)}, s32[6]{0:T(128)}, u32[]{:S(2)}) copy-start(s32[6]{0:T(128)} %cut_x_ref.3) | copy-start | bytes 76
  1.2 15.8 %copy-start.8 = (s32[6]{0:T(128)S(1)}, s32[6]{0:T(128)}, u32[]{:S(2)}) copy-start(s32[6]{0:T(128)} %cut_y_ref.3) | copy-start | bytes 76
  1.3 15.8 %copy-start.10 = (s32[6]{0:T(128)S(1)}, s32[6]{0:T(128)}, u32[]{:S(2)}) copy-start(s32[6]{0:T(128)} %index_ref.1) | copy-start | bytes 76
  1.3 58.1 %copy-start.5 = (f32[256,128]{1,0:T(8,128)S(1)}, f32[256,128]{1,0:T(8,128)}, u32[]{:S(2)}) copy-start(f32[256,128]{1,0:T(8,128)} %constant.125.clone.base_ref) | copy-start | bytes 393220
  1.3 58.1 %copy-start.6 = (f32[16,2,128]{2,1,0:T(2,128)S(1)}, f32[16,2,128]{2,1,0:T(2,128)}, u32[]{:S(2)}) copy-start(f32[16,2,128]{2,1,0:T(2,128)} %constant.126.clone.turn_ref) | copy-start | bytes 49156
  59.4 1.2 %copy-start.1 = (bf16[256,2048]{1,0:T(8,128)(2,1)S(1)}, bf16[256,2048]{1,0:T(8,128)(2,1)}, u32[]{:S(2)}) copy-start(bf16[256,2048]{1,0:T(8,128)(2,1)} %constant.124.clone.1.table_ref) | copy-start | bytes 3145732 | tf_op jit(solution)/shard_map/cond

commit v2 on v1

v2 whole, which is shorter than its diff:
```python
import functools
import math

import jax
import jax.numpy as jnp
import numpy as np
from jax import lax
from jax.experimental import pallas as pl
from jax.experimental.pallas import tpu as pltpu
from jax.sharding import PartitionSpec as P

TABLE = 8
MESH = pl.DeviceIdType.MESH
HIGHEST = lax.Precision.HIGHEST


def box_wave(index, khalf):
    half = index // 2
    return jnp.where(index % 2 == 0, half, jnp.where(index == 1, -khalf, -half))


def wave_tables(positions, length, waves):
    phase = jnp.mod(positions[:, None] * waves[None, :], length).astype(jnp.float32) * (
        2.0 * math.pi / length
    )
    return (jnp.cos(phase), jnp.sin(phase))


def general(field, host, weights, cut_x, cut_y, table_index):
    variables, levels, row_count, ny = field.shape
    owned, kbox = host.shape[0], host.shape[-1]
    fields = variables * levels
    devices = lax.axis_size("row")
    nx = row_count * devices
    place = lax.axis_index("row")
    local_rows = place * row_count + lax.iota(jnp.int32, row_count)
    x_waves = lax.iota(jnp.int32, kbox) - kbox // 2
    y_waves = box_wave(lax.iota(jnp.int32, kbox), kbox // 2)
    own_waves = box_wave(place * owned + lax.iota(jnp.int32, owned), kbox // 2)
    onehot = (table_index[:, None] == lax.iota(jnp.int32, TABLE)[None, :]).astype(jnp.float32)
    blend = jnp.dot(onehot, weights, precision=HIGHEST)
    mask_x = (jnp.abs(x_waves)[None, :] <= cut_x[:, None]).astype(jnp.float32)
    mask_y = (jnp.abs(own_waves)[None, :] <= cut_y[:, None]).astype(jnp.float32)
    scale = blend.T[:, :, None, None] * mask_y[None, :, :, None] * mask_x[None, :, None, :]
    cos_y, sin_y = wave_tables(lax.iota(jnp.int32, ny), ny, y_waves)
    cos_x, sin_x = wave_tables(local_rows, nx, x_waves)
    table_y = jnp.concatenate([cos_y, -sin_y], 1)
    table_x = jnp.stack([jnp.concatenate([cos_x, -sin_x], 1), jnp.concatenate([sin_x, cos_x], 1)])

    def one(pair):
        grid, wanted, factor = pair
        spread = jnp.dot(grid, table_y, precision=HIGHEST).reshape(row_count, 2, kbox)
        parts = jnp.einsum("xck,cxq->kq", spread, table_x, precision=HIGHEST)
        parts = parts.reshape(devices, owned, 2, kbox)
        moved = lax.all_to_all(parts, "row", split_axis=0, concat_axis=0, tiled=True)
        spectrum = jnp.sum(moved, 0) / (nx * ny)
        delta = factor[:, None, :] * (wanted - spectrum)
        box = lax.all_gather(delta, "row", axis=0, tiled=True).reshape(kbox, 2 * kbox)
        back = jnp.einsum("kq,cxq->xck", box, table_x, precision=HIGHEST)
        return grid + jnp.dot(back.reshape(row_count, 2 * kbox), table_y.T, precision=HIGHEST)

    wanted = host.transpose(2, 3, 0, 1, 4).reshape(fields, owned, 2, kbox)
    result = lax.map(
        one, (field.reshape(fields, row_count, ny), wanted, scale.reshape(fields, owned, kbox))
    )
    return result.reshape(field.shape)


def halves(values):
    high = values.astype(jnp.bfloat16)
    return high, (values - high.astype(jnp.float32)).astype(jnp.bfloat16)


def np_halves(values):
    values = values.astype(np.float32)
    high = values.astype(jnp.bfloat16)
    return high, (values - high.astype(np.float32)).astype(jnp.bfloat16)


def real_modes(positions, length, waves, is_sine):
    if isinstance(positions, int):
        positions = np.arange(positions)
    phase = (positions[:, None] * waves[None, :]) % length * (2.0 * np.pi / length)
    return np.where(is_sine[None, :], np.sin(phase), np.cos(phase))


def local_modes(base_ref, turn_ref):
    count = base_ref.shape[0] // 2
    return base_ref[:count] * turn_ref[0, :1] + base_ref[count:] * turn_ref[0, 1:2]


def inverse_kernel(field_ref, modes_ref, table_ref, base_ref, turn_ref, out_ref, three_ref):
    _, count, row_count, ny = field_ref.shape
    kbox = base_ref.shape[1]
    owned = modes_ref.shape[2] // count
    x_high, x_low = halves(local_modes(base_ref, turn_ref))
    x_three = jnp.concatenate([x_high, x_high, x_low], 1)

    @pl.when((pl.program_id(0) == 0) & (pl.program_id(1) == 0))
    def _():
        three_ref[:kbox] = table_ref[:kbox]
        three_ref[kbox:] = table_ref[...]

    parts = []
    for k in range(count):
        high, low = halves(modes_ref[0, :, k * owned : (k + 1) * owned].reshape(kbox, kbox))
        parts.append(
            lax.dot_general(
                x_three,
                jnp.concatenate([high, low, high], 1),
                (((1,), (1,)), ((), ())),
                preferred_element_type=jnp.float32,
            )
        )
    high, low = halves(jnp.concatenate(parts, 0))
    added = jnp.dot(
        jnp.concatenate([high, low, high], 1), three_ref[...], preferred_element_type=jnp.float32
    )
    out_ref[...] = field_ref[...] + added.reshape(field_ref.shape)


def box_kernel(
    bits, chunks, norm, weights_ref, cut_x_ref, cut_y_ref, index_ref, field_ref, table_ref, base_ref,
    turn_ref, host_ref, mix_ref, out_ref, edge_ref, part_ref, full_ref, *scratch
):
    got, kept = scratch[:bits], scratch[bits : 2 * bits]
    send_sem, recv_sem, out_sem = scratch[2 * bits :]
    _, group, row_count, ny = field_ref.shape
    span, kbox = host_ref.shape[-2:]
    owned, khalf, levels = span // group, kbox // 2, cut_x_ref.shape[0]
    half = owned // 2
    now = pl.program_id(0)
    me = lax.axis_index("row")
    member = lax.axis_index("member")
    mine = [(me // (1 << b)) % 2 for b in range(bits)]
    peer = [me + (1 << b) * (1 - 2 * mine[b]) for b in range(bits)]
    barrier = pltpu.get_barrier_semaphore()

    @pl.when(now == 0)
    def _():
        for b in range(bits):
            pl.semaphore_signal(barrier, inc=1, device_id=(member, peer[b]), device_id_type=MESH)
        edge = cut_x_ref[0]
        for level in range(levels):
            edge = jnp.maximum(edge, jnp.maximum(cut_x_ref[level], cut_y_ref[level]))
        edge_ref[0] = edge

    def lead(step, bit_value):
        return (slice(None),) * (bits - 1 - step) + (bit_value,)

    def remote(source, target, stage, chunk, bit):
        return pltpu.make_async_remote_copy(
            src_ref=source,
            dst_ref=target,
            send_sem=send_sem.at[chunk, stage],
            recv_sem=recv_sem.at[chunk, stage],
            device_id=(member, peer[bit]),
            device_id_type=MESH,
        )

    def held(step):
        return part_ref if step == 0 else kept[step - 1]

    def reduce_copy(step, chunk):
        source = held(step).at[(chunk,) + lead(step, 1 - mine[step])]
        return remote(source, got[step].at[chunk], step, chunk, step)

    def gather_copy(step, chunk):
        fixed = tuple(mine[b] for b in range(step, -1, -1))
        block = full_ref.at[(chunk,) + (slice(None),) * (bits - 1 - step) + fixed]
        return remote(block, block, bits + step, chunk, step)

    def out_copy(chunk):
        return pltpu.make_async_copy(full_ref.at[chunk], out_ref.at[chunk], out_sem.at[chunk])

    slot = lax.broadcasted_iota(jnp.int32, (span, kbox), 0)
    column = lax.broadcasted_iota(jnp.int32, (span, kbox), 1)
    line = slot % owned < half

    def swap(values):
        return jnp.where(
            line, pltpu.roll(values, span - half, 0), pltpu.roll(values, half, 0)
        )

    def mixed(values, axis):
        total = 0.0
        for _ in range(3):
            piece = values.astype(jnp.bfloat16)
            values = values - piece.astype(jnp.float32)
            total = total + lax.dot_general(
                piece,
                mix_ref[...],
                (((1,), (axis,)), ((), ())),
                preferred_element_type=jnp.float32,
            )
        return total

    def pull(chunk):
        both = mixed(kept[bits - 1][chunk] * norm, 0)
        even, odd = both[:, :kbox], both[:, kbox:]
        even_s, odd_s = swap(even), swap(odd)
        real = jnp.where(line, even - odd_s, even_s + odd)
        imag = jnp.where(line, -(odd + even_s), even - odd_s)
        wave = me * half + slot % half
        wave = jnp.where((wave == 0) & (slot % owned >= half), khalf, wave)
        steps = levels // group
        scale = jnp.zeros((span, kbox), jnp.float32)
        for k in range(group):
            level = (chunk % steps) * group + k
            inside = (jnp.abs(column - khalf) <= cut_x_ref[level]) & (wave <= cut_y_ref[level])
            blend = jnp.where(inside, weights_ref[index_ref[level], chunk // steps], 0.0)
            scale = jnp.where(slot // owned == k, blend, scale)
        real = scale * (host_ref[0, chunk] - real)
        imag = scale * (host_ref[1, chunk] - imag)
        real_s, imag_s = swap(real), swap(imag)
        cosine = jnp.where(line, real + real_s, imag - imag_s)
        sine = jnp.where(line, -(imag + imag_s), real - real_s)
        own = tuple(mine[b] for b in range(bits - 1, -1, -1))
        full_ref[(chunk,) + own] = mixed(jnp.concatenate([cosine, sine], 1), 1)

    def advance(stage, chunk):
        if stage < bits:
            reduce_copy(stage, chunk).wait()
            own = held(stage)[(chunk,) + lead(stage, mine[stage])]
            kept[stage][chunk] = own + got[stage][chunk]
            if stage + 1 < bits:
                reduce_copy(stage + 1, chunk).start()
            else:
                pull(chunk)
                gather_copy(bits - 1, chunk).start()
        else:
            step = 2 * bits - 1 - stage
            gather_copy(step, chunk).wait()
            if step > 0:
                gather_copy(step - 1, chunk).start()
            else:
                out_copy(chunk).start()

    @pl.when(now < chunks)
    def _():
        high, low = halves(field_ref[...].reshape(group * row_count, ny))
        both = jnp.dot(high, table_ref[...], preferred_element_type=jnp.float32)
        rest = jnp.dot(low, table_ref[:, :kbox], preferred_element_type=jnp.float32)
        part = both[:, :kbox] + both[:, kbox:] + rest
        x_high, x_low = halves(local_modes(base_ref, turn_ref))
        x_three = jnp.concatenate([x_high, x_high, x_low], 0)
        cube = (2,) * bits
        for k in range(group):
            high, low = halves(part[k * row_count : (k + 1) * row_count])
            moded = lax.dot_general(
                jnp.concatenate([high, low, high], 0),
                x_three,
                (((0,), (0,)), ((), ())),
                preferred_element_type=jnp.float32,
            )
            where = (now,) + (slice(None),) * bits + (slice(k * owned, (k + 1) * owned),)
            part_ref[where] = moded.reshape(cube + (owned, kbox))

    @pl.when(now == 0)
    def _():
        pl.semaphore_wait(barrier, bits)

    for stage in range(2 * bits - 1, -1, -1):
        chunk = now - 1 - stage

        @pl.when((chunk >= 0) & (chunk < chunks))
        def _(stage=stage, chunk=chunk):
            advance(stage, chunk)

    @pl.when(now < chunks)
    def _():
        reduce_copy(0, now).start()

    @pl.when(now == pl.num_programs(0) - 1)
    def _():
        for chunk in range(chunks):
            out_copy(chunk).wait()


def box_modes(scalars, field, table, base, turn, host, mix, group):
    variables, levels, row_count, ny = field.shape
    devices, kbox = turn.shape[0], host.shape[-1]
    chunks, span = host.shape[1:3]
    steps = levels // group
    bits = devices.bit_length() - 1
    cube = (2,) * bits
    sizes = [
        pltpu.VMEM((chunks,) + (2,) * (bits - 1 - step) + (span, kbox), jnp.float32)
        for step in range(bits)
    ]

    def chunk_at(now):
        chunk = jnp.minimum(now, chunks - 1)
        return (chunk // steps, chunk % steps, 0, 0)

    def whole(array):
        return pl.BlockSpec(array.shape, lambda now: (0,) * array.ndim)

    smem = pl.BlockSpec(memory_space=pltpu.SMEM)
    return pl.pallas_call(
        functools.partial(box_kernel, bits, chunks, 1.0 / (row_count * devices * ny)),
        grid=(chunks + 2 * bits,),
        out_shape=(
            jax.ShapeDtypeStruct((chunks,) + cube + (span, kbox), jnp.float32),
            jax.ShapeDtypeStruct((1,), jnp.int32),
        ),
        in_specs=[smem] * 4
        + [
            pl.BlockSpec((1, group, row_count, ny), chunk_at),
            whole(table),
            whole(base),
            pl.BlockSpec((1, 2, kbox), lambda now: (lax.axis_index("row"), 0, 0)),
            whole(host),
            whole(mix),
        ],
        out_specs=(pl.BlockSpec(memory_space=pl.ANY), smem),
        scratch_shapes=[pltpu.VMEM((chunks,) + cube + (span, kbox), jnp.float32)] * 2
        + sizes * 2
        + [
            pltpu.SemaphoreType.DMA((chunks, 2 * bits)),
            pltpu.SemaphoreType.DMA((chunks, 2 * bits)),
            pltpu.SemaphoreType.DMA((chunks,)),
        ],
        compiler_params=pltpu.CompilerParams(
            collective_id=0, has_side_effects=True, vmem_limit_bytes=48 * 1024 * 1024
        ),
    )(*scalars, field, table, base, turn, host, mix)


def nudge(field, host, weights, cut_x, cut_y, table_index):
    variables, levels, row_count, ny = field.shape
    owned, kbox = host.shape[0], host.shape[-1]
    khalf, half = kbox // 2, owned // 2
    devices = lax.axis_size("row")
    nx = row_count * devices
    fields = variables * levels

    column = np.arange(kbox)
    y_wave = column // owned * half + column % half
    y_sine = column % owned >= half
    y_high, y_low = np_halves(real_modes(ny, ny, y_wave, y_sine))
    table_y = jnp.asarray(np.concatenate([y_high, y_low], 1))
    table_back = jnp.asarray(np.concatenate([y_high.T, y_low.T], 0))
    x_wave, x_sine = column % khalf, column >= khalf
    start = np.arange(devices) * row_count
    base = np.concatenate(
        [real_modes(row_count, nx, x_wave, column < 0), real_modes(row_count, nx, x_wave, column >= 0)]
    )
    turn_cos = real_modes(start, nx, x_wave, column < 0)
    turn_sin = real_modes(start, nx, x_wave, column >= 0)
    turn = np.stack(
        [np.where(x_sine, turn_sin, turn_cos), np.where(x_sine, turn_cos, -turn_sin)], 1
    )
    base = jnp.asarray(base.astype(np.float32))
    turn = jnp.asarray(turn.astype(np.float32))
    wave = column - khalf
    inside = np.abs(wave) < khalf
    mc = ((column[:, None] == np.abs(wave)[None, :]) & inside).astype(np.float32)
    ms = ((column[:, None] == np.abs(wave)[None, :] + khalf) & inside) * np.sign(wave)
    ms = ms.astype(np.float32)

    group = math.gcd(levels, 3)
    steps = levels // group
    grid_block = pl.BlockSpec((1, group, row_count, ny), lambda v, g: (v, g, 0, 0))
    span = group * owned
    mode_block = pl.BlockSpec(
        (1, devices, span, kbox), lambda v, g: (v * steps + g, 0, 0, 0)
    )

    def whole(*shape):
        return pl.BlockSpec(shape, lambda v, g: (0,) * len(shape))

    local_turn = pl.BlockSpec((1, 2, kbox), lambda v, g: (lax.axis_index("row"), 0, 0))
    params = pltpu.CompilerParams(vmem_limit_bytes=48 * 1024 * 1024)
    placed = host.reshape(half, 2, 2, fields, kbox).transpose(2, 3, 1, 0, 4)
    modes, edge = box_modes(
        (weights, cut_x, cut_y, table_index),
        field,
        table_y,
        base,
        turn,
        placed.reshape(2, fields // group, span, kbox),
        jnp.asarray(np.concatenate([mc, ms], 1)).astype(jnp.bfloat16),
        group,
    )
    modes = modes.reshape(fields // group, devices, span, kbox)

    inverse = pl.pallas_call(
        inverse_kernel,
        grid=(variables, steps),
        out_shape=jax.ShapeDtypeStruct(field.shape, jnp.float32),
        in_specs=[grid_block, mode_block, whole(2 * kbox, ny), whole(2 * row_count, kbox), local_turn],
        out_specs=grid_block,
        scratch_shapes=[pltpu.VMEM((3 * kbox, ny), jnp.bfloat16)],
        compiler_params=params,
    )
    return lax.cond(
        edge[0] >= khalf,
        lambda *args: general(*args[:6]),
        lambda *args: inverse(args[0], *args[6:]),
        field, host, weights, cut_x, cut_y, table_index, modes, table_back, base, turn,
    )


def solution(mesh):
    return jax.shard_map(
        nudge,
        mesh=mesh,
        in_specs=(
            P("member", None, "row", None),
            P("row", None, "member", None, None),
            P(),
            P(),
            P(),
            P(),
        ),
        out_specs=P("member", None, "row", None),
        check_vma=False,
    )
```

time: 82.9 us -> 84.2 us (1.016)
  local copies, waits for them, and re-layouts: 2.69 us -> 5.18 us
  Pallas kernels: 79 us -> 77.8 us
    unnamed x22 -> x20, local copies, waits for them, and re-layouts: 1.41 us -> 3.91 us
    pallas_call x2 -> x1, Pallas kernels: 57.1 us -> 55.9 us  [box_modes(): pl.pallas_call(functools.partial(box_kernel, bits, chunks, 1.0 / (row_cou...]
where the time goes in v2:
time: 84.2 us; the launch traced here: 83.8 us
  Pallas kernels  77.8 us (92%)
  local copies, waits for them, and re-layouts  5.18 us (6%)
    pallas_call x1, Pallas kernels, box_modes(): pl.pallas_call(functools.partial(box_kernel, bits, chunks, 1.0 / (row_cou...  55.9 us
    pallas_call x1, Pallas kernels, nudge(): inverse(args[0], *args[6:])  21.8 us
    unnamed x20, local copies, waits for them, and re-layouts  3.91 us

profile of v2, /device:TPU:0, one launch (start us, length us, event | category | flops | bytes accessed | tf_op | source)
XLA Modules:
  0.0 83.8 jit_solution(10552180099142718784)
XLA Ops:
  0.0 0.0 copy-start.4
  0.0 0.0 copy-start.5
  0.0 0.0 copy-start.3
  0.0 0.0 copy-start.8
  0.0 0.0 copy-start.6
  0.0 0.0 copy-start.7
  0.0 0.0 copy-start.9
  0.0 1.1 %copy.25 = f32[8,2,4,6,128]{4,0,3,2,1:T(8,128)S(1)} copy(f32[8,2,4,6,128]{4,2,3,1,0:T(4,128)} %param.16) | data formatting | bytes 393216 | tf_op args[1]
  1.1 0.1 copy.26
  1.2 0.8 copy.27.weights_ref
  1.9 0.0 copy-start
  1.9 1.2 %copy-done = bf16[2048,256]{1,0:T(8,128)(2,1)S(1)} copy-done((bf16[2048,256]{1,0:T(8,128)(2,1)S(1)}, bf16[2048,256]{1,0:T(8,128)(2,1)}, u32[]{:S(2)}) %copy-start) | copy-done | bytes 1048600
  3.1 0.0 copy-start.2
  3.1 0.8 copy-done.2
  4.0 55.9 %shard_map.112 = (f32[8,2,2,2,2,24,128]{6,5,4,3,2,1,0:T(8,128)S(1)}, s32[1]{0:T(128)}) custom-call(f32[8,4]{1,0:T(8,128)S(1)} %copy.27.weights_ref, s32[6]{0:T(128)} %cut_x_ref.1, s32[6]{0:T(128)} %cut_y_ref.1, s32[6]{0:T(128)} %index_ref.1, f32[4,6,128,2048]{3,2,1,0:T(8,128)} %field_ref.1, bf16[2048,256]{1,0:T(8,128)(2,1)S(1)} %copy-done, ...), custom_call_target="tpu_custom_call" | custom-call | tf_op jit(solution)/shard_map/pallas_call | solution.py:300
  60.6 0.0 copy-done.4
  60.6 0.0 copy-done.5
  60.6 0.0 copy-done.3
  60.6 0.0 copy-done.8
  60.6 0.0 copy-done.6
  60.6 0.0 copy-done.7
  60.7 0.0 copy-done.9
  60.7 23.1 %conditional.1 = (f32[4,6,128,2048]{3,2,1,0:T(8,128)}) conditional(s32[]{:T(128)} %bitcast.22, (f32[4,6,128,2048]{3,2,1,0:T(8,128)}, f32[8,2,2,2,2,24,128]{6,5,4,3,2,1,0:T(8,128)S(1)}, (), f32[256,128]{1,0:T(8,128)S(1)}, f32[16,2,128]{2,1,0:T(2,128)S(1)}) %tuple.45, (f32[4,6,128,2048]{3,2,1,0:T(8,128)}, f32[8,2,4,6,128]{4,2,3,1,0:T(4,128)S(1)}, ...), branch_computations={%region_0.0_spmd, %region_1.5_spmd} | conditional | flops 1817103232 | bytes 17667372 | solution.py:397
  60.7 0.0 copy-start.1
  60.7 1.2 %copy-done.1 = bf16[256,2048]{1,0:T(8,128)(2,1)S(1)} copy-done((bf16[256,2048]{1,0:T(8,128)(2,1)S(1)}, bf16[256,2048]{1,0:T(8,128)(2,1)}, u32[]{:S(2)}) %copy-start.1) | copy-done | bytes 1048600 | tf_op jit(solution)/shard_map/cond
  61.9 21.8 %branch_0_fun.1 = f32[4,6,128,2048]{3,2,1,0:T(8,128)} custom-call(f32[4,6,128,2048]{3,2,1,0:T(8,128)} %get-tuple-element.58.field_ref, f32[8,16,24,128]{3,2,1,0:T(8,128)S(1)} %bitcast.87, bf16[256,2048]{1,0:T(8,128)(2,1)S(1)} %copy-done.1, f32[256,128]{1,0:T(8,128)S(1)} %get-tuple-element.61.base_ref, f32[16,2,128]{2,1,0:T(2,128)S(1)} %get-tuple-element.62.turn_ref), custom_call_target="tpu_custom_call" | custom-call | tf_op jit(solution)/shard_map/cond/branch_0_fun/pallas_call | solution.py:400
Async XLA Ops:
  0.0 60.6 %copy-start.4 = (f32[256,128]{1,0:T(8,128)S(1)}, f32[256,128]{1,0:T(8,128)}, u32[]{:S(2)}) copy-start(f32[256,128]{1,0:T(8,128)} %constant.123.clone.base_ref) | copy-start | bytes 393220
  0.0 60.6 %copy-start.5 = (f32[16,2,128]{2,1,0:T(2,128)S(1)}, f32[16,2,128]{2,1,0:T(2,128)}, u32[]{:S(2)}) copy-start(f32[16,2,128]{2,1,0:T(2,128)} %constant.124.clone.turn_ref) | copy-start | bytes 49156
  0.0 60.6 %copy-start.3 = (f32[8,2,4,6,128]{4,2,3,1,0:T(4,128)S(1)}, f32[8,2,4,6,128]{4,2,3,1,0:T(4,128)}, u32[]{:S(2)}) copy-start(f32[8,2,4,6,128]{4,2,3,1,0:T(4,128)} %param.16) | copy-start | bytes 589828
  0.0 60.6 %copy-start.8 = (f32[8,4]{0,1:T(4,128)S(1)}, f32[8,4]{0,1:T(4,128)}, u32[]{:S(2)}) copy-start(f32[8,4]{0,1:T(4,128)} %param.17) | copy-start | bytes 388
  0.0 60.6 %copy-start.6 = (s32[6]{0:T(128)S(1)}, s32[6]{0:T(128)}, u32[]{:S(2)}) copy-start(s32[6]{0:T(128)} %cut_x_ref.1) | copy-start | bytes 76
  0.0 60.6 %copy-start.7 = (s32[6]{0:T(128)S(1)}, s32[6]{0:T(128)}, u32[]{:S(2)}) copy-start(s32[6]{0:T(128)} %cut_y_ref.1) | copy-start | bytes 76
  0.0 60.6 %copy-start.9 = (s32[6]{0:T(128)S(1)}, s32[6]{0:T(128)}, u32[]{:S(2)}) copy-start(s32[6]{0:T(128)} %index_ref.1) | copy-start | bytes 76
  1.9 1.2 %copy-start = (bf16[2048,256]{1,0:T(8,128)(2,1)S(1)}, bf16[2048,256]{1,0:T(8,128)(2,1)}, u32[]{:S(2)}) copy-start(bf16[2048,256]{1,0:T(8,128)(2,1)} %constant.121.clone.table_ref) | copy-start | bytes 3145732
  3.1 0.8 %copy-start.2 = (bf16[128,256]{1,0:T(8,128)(2,1)S(1)}, bf16[128,256]{1,0:T(8,128)(2,1)}, u32[]{:S(2)}) copy-start(bf16[128,256]{1,0:T(8,128)(2,1)} %constant.127.mix_ref) | copy-start | bytes 196612
  60.7 1.2 %copy-start.1 = (bf16[256,2048]{1,0:T(8,128)(2,1)S(1)}, bf16[256,2048]{1,0:T(8,128)(2,1)}, u32[]{:S(2)}) copy-start(bf16[256,2048]{1,0:T(8,128)(2,1)} %constant.122.clone.1.table_ref) | copy-start | bytes 3145732 | tf_op jit(solution)/shard_map/cond

commit v3 on v2

--- a/solution.py
+++ b/solution.py
@@ -11,6 +11,7 @@
 
 TABLE = 8
 MESH = pl.DeviceIdType.MESH
+VMEM_BYTES = 63_000_000
 HIGHEST = lax.Precision.HIGHEST
 
 
@@ -119,6 +120,10 @@
     out_ref[...] = field_ref[...] + added.reshape(field_ref.shape)
 
 
+def stage_step(stage):
+    return 2 * stage + 1
+
+
 def box_kernel(
     bits, chunks, norm, weights_ref, cut_x_ref, cut_y_ref, index_ref, field_ref, table_ref, base_ref,
     turn_ref, host_ref, mix_ref, out_ref, edge_ref, part_ref, full_ref, *scratch
@@ -208,7 +213,7 @@
         for k in range(group):
             level = (chunk % steps) * group + k
             inside = (jnp.abs(column - khalf) <= cut_x_ref[level]) & (wave <= cut_y_ref[level])
-            blend = jnp.where(inside, weights_ref[index_ref[level], chunk // steps], 0.0)
+            blend = jnp.where(inside, weights_ref[chunk // steps, index_ref[level]], 0.0)
             scale = jnp.where(slot // owned == k, blend, scale)
         real = scale * (host_ref[0, chunk] - real)
         imag = scale * (host_ref[1, chunk] - imag)
@@ -260,8 +265,8 @@
     def _():
         pl.semaphore_wait(barrier, bits)
 
-    for stage in range(2 * bits - 1, -1, -1):
-        chunk = now - 1 - stage
+    for stage in range(2 * bits):
+        chunk = now - stage_step(stage)
 
         @pl.when((chunk >= 0) & (chunk < chunks))
         def _(stage=stage, chunk=chunk):
@@ -299,7 +304,7 @@
     smem = pl.BlockSpec(memory_space=pltpu.SMEM)
     return pl.pallas_call(
         functools.partial(box_kernel, bits, chunks, 1.0 / (row_count * devices * ny)),
-        grid=(chunks + 2 * bits,),
+        grid=(chunks + stage_step(2 * bits - 1),),
         out_shape=(
             jax.ShapeDtypeStruct((chunks,) + cube + (span, kbox), jnp.float32),
             jax.ShapeDtypeStruct((1,), jnp.int32),
@@ -322,7 +327,7 @@
             pltpu.SemaphoreType.DMA((chunks,)),
         ],
         compiler_params=pltpu.CompilerParams(
-            collective_id=0, has_side_effects=True, vmem_limit_bytes=48 * 1024 * 1024
+            collective_id=0, has_side_effects=True, vmem_limit_bytes=VMEM_BYTES
         ),
     )(*scalars, field, table, base, turn, host, mix)
 
@@ -359,7 +364,7 @@
     ms = ((column[:, None] == np.abs(wave)[None, :] + khalf) & inside) * np.sign(wave)
     ms = ms.astype(np.float32)
 
-    group = math.gcd(levels, 3)
+    group = levels
     steps = levels // group
     grid_block = pl.BlockSpec((1, group, row_count, ny), lambda v, g: (v, g, 0, 0))
     span = group * owned
@@ -371,10 +376,10 @@
         return pl.BlockSpec(shape, lambda v, g: (0,) * len(shape))
 
     local_turn = pl.BlockSpec((1, 2, kbox), lambda v, g: (lax.axis_index("row"), 0, 0))
-    params = pltpu.CompilerParams(vmem_limit_bytes=48 * 1024 * 1024)
+    params = pltpu.CompilerParams(vmem_limit_bytes=VMEM_BYTES)
     placed = host.reshape(half, 2, 2, fields, kbox).transpose(2, 3, 1, 0, 4)
     modes, edge = box_modes(
-        (weights, cut_x, cut_y, table_index),
+        (weights.T, cut_x, cut_y, table_index),
         field,
         table_y,
         base,

time: 84.2 us -> 65.3 us (0.78)
  Pallas kernels: 77.8 us -> 62.5 us
  local copies, waits for them, and re-layouts: 5.18 us -> 1.82 us
    pallas_call x1, Pallas kernels: 55.9 us -> 43.3 us  [box_modes(): pl.pallas_call(functools.partial(box_kernel, bits, chunks, 1.0 / (row_cou...]
    unnamed x20 -> x15, local copies, waits for them, and re-layouts: 3.91 us -> 1.09 us
    pallas_call x1, Pallas kernels: 21.8 us -> 19.2 us  [nudge(): inverse(args[0], *args[6:])]
    cond x2 -> x0, local copies, waits for them, and re-layouts: 1.22 us -> none
where the time goes in v3:
time: 65.3 us; the launch traced here: 65.1 us
  Pallas kernels  62.5 us (96%)
  local copies, waits for them, and re-layouts  1.82 us (3%)
  between operations  0.71 us (1%)
    pallas_call x1, Pallas kernels, box_modes(): pl.pallas_call(functools.partial(box_kernel, bits, chunks, 1.0 / (row_cou...  43.3 us
    pallas_call x1, Pallas kernels, nudge(): inverse(args[0], *args[6:])  19.2 us

profile of v3, /device:TPU:0, one launch (start us, length us, event | category | flops | bytes accessed | tf_op | source)
XLA Modules:
  0.0 65.1 jit_solution(16496786453910984344)
XLA Ops:
  0.0 0.0 copy-start.1
  0.0 0.0 copy-start.2
  0.0 0.0 copy-start
  0.0 0.0 copy-start.3
  0.0 0.0 copy-start.4
  0.0 0.0 copy-start.5
  0.0 0.0 copy-start.6
  0.0 1.1 %copy.23 = f32[8,2,4,6,128]{4,0,3,2,1:T(8,128)S(1)} copy(f32[8,2,4,6,128]{4,2,3,1,0:T(4,128)} %param.16) | data formatting | bytes 393216 | tf_op args[1]
  1.1 0.7 %copy.24 = f32[2,24,2,4,128]{4,3,2,1,0:T(4,128)} copy(f32[2,24,2,4,128]{4,2,3,1,0:T(2,128)S(1)} %bitcast.89) | data formatting | bytes 393216 | tf_op jit(solution)/shard_map/transpose | solution.py:380
  1.8 43.3 %shard_map.112 = (f32[4,2,2,2,2,48,128]{6,5,4,3,2,1,0:T(8,128)S(1)}, s32[1]{0:T(128)}) custom-call(f32[4,8]{1,0:T(4,128)} %bitcast.91, s32[6]{0:T(128)} %cut_x_ref.1, s32[6]{0:T(128)} %cut_y_ref.1, s32[6]{0:T(128)} %index_ref.1, f32[4,6,128,2048]{3,2,1,0:T(8,128)} %field_ref.1, bf16[2048,256]{1,0:T(8,128)(2,1)} %constant.121.clone.table_ref, ...), custom_call_target="tpu_custom_call" | custom-call | tf_op jit(solution)/shard_map/pallas_call | solution.py:305
  45.8 0.0 copy-done.1
  45.8 0.0 copy-done.2
  45.8 0.0 copy-done
  45.8 0.0 copy-done.3
  45.8 0.0 copy-done.4
  45.8 0.0 copy-done.5
  45.8 0.0 copy-done.6
  45.9 19.2 %conditional.1 = (f32[4,6,128,2048]{3,2,1,0:T(8,128)}) conditional(s32[]{:T(128)} %bitcast.23, (f32[4,6,128,2048]{3,2,1,0:T(8,128)}, f32[4,2,2,2,2,48,128]{6,5,4,3,2,1,0:T(8,128)S(1)}, (), f32[256,128]{1,0:T(8,128)S(1)}, f32[16,2,128]{2,1,0:T(2,128)S(1)}) %tuple.45, (f32[4,6,128,2048]{3,2,1,0:T(8,128)}, f32[8,2,4,6,128]{4,2,3,1,0:T(4,128)S(1)}, ...), branch_computations={%region_0.0_spmd, %region_1.5_spmd} | conditional | flops 1817103232 | bytes 17667372 | solution.py:402
  45.9 19.2 %branch_0_fun.1 = f32[4,6,128,2048]{3,2,1,0:T(8,128)} custom-call(f32[4,6,128,2048]{3,2,1,0:T(8,128)} %get-tuple-element.58.field_ref, f32[4,16,48,128]{3,2,1,0:T(8,128)S(1)} %bitcast.87, bf16[256,2048]{1,0:T(8,128)(2,1)} %constant.122.clone.1.table_ref, f32[256,128]{1,0:T(8,128)S(1)} %get-tuple-element.61.base_ref, f32[16,2,128]{2,1,0:T(2,128)S(1)} %get-tuple-element.62.turn_ref), custom_call_target="tpu_custom_call" | custom-call | tf_op jit(solution)/shard_map/cond/branch_0_fun/pallas_call | solution.py:405
Async XLA Ops:
  0.0 45.8 %copy-start.1 = (f32[256,128]{1,0:T(8,128)S(1)}, f32[256,128]{1,0:T(8,128)}, u32[]{:S(2)}) copy-start(f32[256,128]{1,0:T(8,128)} %constant.123.clone.base_ref) | copy-start | bytes 393220
  0.0 45.8 %copy-start.2 = (f32[16,2,128]{2,1,0:T(2,128)S(1)}, f32[16,2,128]{2,1,0:T(2,128)}, u32[]{:S(2)}) copy-start(f32[16,2,128]{2,1,0:T(2,128)} %constant.124.clone.turn_ref) | copy-start | bytes 49156
  0.0 45.8 %copy-start = (f32[8,2,4,6,128]{4,2,3,1,0:T(4,128)S(1)}, f32[8,2,4,6,128]{4,2,3,1,0:T(4,128)}, u32[]{:S(2)}) copy-start(f32[8,2,4,6,128]{4,2,3,1,0:T(4,128)} %param.16) | copy-start | bytes 589828
  0.0 45.8 %copy-start.3 = (f32[8,4]{0,1:T(4,128)S(1)}, f32[8,4]{0,1:T(4,128)}, u32[]{:S(2)}) copy-start(f32[8,4]{0,1:T(4,128)} %param.17) | copy-start | bytes 388
  0.0 45.8 %copy-start.4 = (s32[6]{0:T(128)S(1)}, s32[6]{0:T(128)}, u32[]{:S(2)}) copy-start(s32[6]{0:T(128)} %cut_x_ref.1) | copy-start | bytes 76
  0.0 45.8 %copy-start.5 = (s32[6]{0:T(128)S(1)}, s32[6]{0:T(128)}, u32[]{:S(2)}) copy-start(s32[6]{0:T(128)} %cut_y_ref.1) | copy-start | bytes 76
  0.0 45.8 %copy-start.6 = (s32[6]{0:T(128)S(1)}, s32[6]{0:T(128)}, u32[]{:S(2)}) copy-start(s32[6]{0:T(128)} %index_ref.1) | copy-start | bytes 76
